TPU v7x, 32 devices: a whole 2x2x4 slice. The times are simulated.
32 devices in a mesh: group: 8 (over z, x), peer: 4 (over y, core).
Axes of the slice: x: 2, y: 2, z: 4, core: 2. Of those that a mesh axis runs over, the one named last changes fastest.
Arguments:
- features: bfloat16 [12288, 1024], P(('group', 'peer')), may hold values from -6 to 6
- task_mask: int32 [12288], P(('group', 'peer')), may hold values from 0 to 65535, as said below
- tower_in: bfloat16 [16, 2048, 1024], P('peer', 'group'), may hold values from -0.1875 to 0.1875
- tower_bias: bfloat16 [16, 2048], P('peer', 'group'), may hold values from -5 to 5
- tower_head: bfloat16 [16, 2048], P('peer', 'group'), may hold values from -0.125 to 0.125
- head_bias: float32 [16], P('peer'), may hold values from -4 to 4
Outputs:
- predictions: float32 [12288, 16], P(('group', 'peer'))
Inputs may be any that keep to these rules, and one draw needn't show every extreme that they name: `task_mask`: only bits 0 to 15 are used. Among the 384 samples of one device (aligned blocks of 384), at most 176 have any one bit set; in every run of 4 blocks that one group holds, some task's bit is set exactly 176 times in each block.
All inputs are finite; a program needn't handle non-finite values.
Results may differ from a plain program's by a relative error of at most 0.0003.
Values may be sent and summed in bfloat16 or wider, within the bound.
A program may use at most 128 MiB of HBM per device.

v0:
```python
import jax
import jax.numpy as jnp
from jax import lax
from jax.sharding import PartitionSpec as P

CAP = 176


def shards(features, task_mask, tower_in, tower_bias, tower_head, head_bias):
    peers = lax.axis_size("peer")
    local_tasks = tower_in.shape[0]
    all_tasks = local_tasks * peers
    task_ids = jnp.arange(all_tasks, dtype=jnp.int32)
    slot_indices = jnp.arange(CAP, dtype=jnp.int32)
    task_bits = task_mask[:, None] >> task_ids[None, :] & 1
    inclusive = jnp.cumsum(task_bits, axis=0)
    slot_rank = inclusive - task_bits
    task_selector = (slot_rank.T[:, None, :] == slot_indices[None, :, None]) & (
        task_bits.T[:, None, :] == 1
    )
    outgoing = jnp.einsum(
        "yra,az->yrz",
        task_selector.astype(jnp.bfloat16),
        features,
        preferred_element_type=jnp.float32,
    ).astype(jnp.bfloat16)
    outgoing = outgoing.reshape(peers, local_tasks, CAP, features.shape[1])
    arrived = lax.all_to_all(outgoing, "peer", split_axis=0, concat_axis=0, tiled=True)
    weight = lax.all_gather(tower_in, "group", axis=1, tiled=True)
    hidden_unit_bias = lax.all_gather(tower_bias, "group", axis=1, tiled=True)
    head_row = lax.all_gather(tower_head, "group", axis=1, tiled=True)
    preact = jnp.einsum("sjcd,jhd->sjch", arrived, weight, preferred_element_type=jnp.float32)
    hidden = jnp.maximum(preact + hidden_unit_bias.astype(jnp.float32)[None, :, None, :], 0.0)
    logits = jnp.einsum(
        "sjch,jh->sjc", hidden, head_row.astype(jnp.float32), precision=lax.Precision.HIGHEST
    )
    logits = logits + head_bias[None, :, None]
    returned_output = lax.all_to_all(
        logits, "peer", split_axis=0, concat_axis=0, tiled=True
    ).reshape(all_tasks, CAP)
    task_selector = (slot_rank.T[:, None, :] == slot_indices[None, :, None]) & (
        task_bits.T[:, None, :] == 1
    )
    return jnp.einsum(
        "ivf,iv->fi",
        task_selector.astype(jnp.float32),
        returned_output,
        precision=lax.Precision.HIGHEST,
    )


def solution(mesh):
    placed = (
        P(("group", "peer"), None),
        P(("group", "peer")),
        P("peer", "group", None),
        P("peer", "group"),
        P("peer", "group"),
        P("peer"),
    )
    return jax.shard_map(
        shards, mesh=mesh, in_specs=placed, out_specs=P(("group", "peer"), None), check_vma=False
    )
```

profile of v0, /device:TPU:0, one launch (start us, length us, event | category | flops | bytes accessed | tf_op | source)
XLA Modules:
  0.0 291.0 jit_solution(16052179998820379908)
XLA Ops:
  6.5 0.0 copy-start
  6.5 0.0 all-gather.2.cloned.1.call-start
  6.5 0.7 all-gather.2.cloned.1.call-update
  7.3 0.7 shift-right-arithmetic_and_fusion.1
  7.9 0.9 reduce-window.6
  8.8 0.2 slice_reduce_fusion
  9.1 0.7 fusion.23
  9.8 0.8 bitcast_subtract_fusion
  10.5 0.0 copy-done
  10.5 4.9 %fusion.14 = bf16[16,176,1024]{2,1,0:T(8,128)(2,1)} fusion(s32[16,384]{1,0:T(8,128)S(1)} %bitcast_subtract_fusion, pred[16,384]{1,0:T(8,128)(4,1)S(1)} %fusion.23, bf16[384,1024]{1,0:T(8,128)(2,1)S(1)} %copy-done), kind=kOutput, calls=%fused_computation.13 | convolution fusion | flops 2219638784 | bytes 6584320 | tf_op jit(solution)/shard_map/yra,az->yrz/dot_general | solution.py:21
  15.4 0.0 copy-start.1
  15.4 0.0 copy-start.2
  15.4 5.3 %all-to-all-start = ((bf16[4,4,176,1024]{3,2,1,0:T(8,128)(2,1)}), bf16[4,4,176,1024]{3,2,1,0:T(8,128)(2,1)}, u32[]{:S(2)}, u32[]{:S(2)}) async-start(bf16[4,4,176,1024]{3,2,1,0:T(8,128)(2,1)} %bitcast.32), calls=%async_computation | async-start | bytes 11534336 | tf_op jit(solution)/shard_map/all_to_all | solution.py:28
  20.7 0.0 copy-done.1
  20.7 29.4 %all_gather.10 = bf16[4,2048]{1,0:T(4,128)(2,1)S(1)} all-gather(bf16[4,256]{1,0:T(4,128)(2,1)S(1)} %copy-done.1), channel_id=1, replica_groups=mesh['group'=8,'peer'=4] {'group'}, dimensions={1}, use_global_device_ids=true | all-gather | bytes 18432 | tf_op jit(solution)/shard_map/all_gather | solution.py:30
  50.2 0.0 copy-done.2
  50.2 27.3 %all_gather.11 = bf16[4,2048]{1,0:T(4,128)(2,1)S(1)} all-gather(bf16[4,256]{1,0:T(4,128)(2,1)S(1)} %copy-done.2), channel_id=1, replica_groups=mesh['group'=8,'peer'=4] {'group'}, dimensions={1}, use_global_device_ids=true | all-gather | bytes 18432 | tf_op jit(solution)/shard_map/all_gather | solution.py:31
  77.5 9.2 %all-to-all-done = bf16[4,4,176,1024]{3,2,1,0:T(8,128)(2,1)} async-done(((bf16[4,4,176,1024]{3,2,1,0:T(8,128)(2,1)}), bf16[4,4,176,1024]{3,2,1,0:T(8,128)(2,1)}, u32[]{:S(2)}, u32[]{:S(2)}) %all-to-all-start) | async-done | bytes 5767200 | tf_op jit(solution)/shard_map/all_to_all | solution.py:28
  86.7 153.3 %all-gather.2.cloned.1.call-done = bf16[4,2048,1024]{2,1,0:T(8,128)(2,1)} async-done(((bf16[4,256,1024]{2,1,0:T(8,128)(2,1)}), bf16[4,2048,1024]{2,1,0:T(8,128)(2,1)}) %all-gather.2.cloned.1.call-update) | async-done | bytes 16777232 | tf_op jit(solution)/shard_map/all_gather | solution.py:29
  240.0 20.6 %fusion.4 = f32[4,4,176,2048]{3,2,1,0:T(8,128)} fusion(bf16[4,2048,1024]{2,1,0:T(8,128)(2,1)} %all-gather.2.cloned.1.call-done, bf16[4,4,176,1024]{3,2,1,0:T(8,128)(2,1)} %all-to-all-done), kind=kOutput, calls=%fused_computation.4 | convolution fusion | flops 11811160064 | bytes 45613056 | tf_op jit(solution)/shard_map/sjcd,jhd->sjch/dot_general | solution.py:32
  260.6 0.0 copy-start.3
  260.6 14.7 %fusion = f32[4,1,4,176]{3,1,2,0:T(1,128)S(1)} fusion(f32[4,4,176,2048]{3,2,1,0:T(8,128)} %fusion.4, f32[4,2048]{1,0:T(4,128)S(1)} %convert_element_type.10, bf16[4,2048,1,1]{1,0,2,3:T(4,128)(2,1)S(1)} %bitcast.33), kind=kOutput, calls=%fused_computation | convolution fusion | flops 80740352 | bytes 23129088 | tf_op jit(solution)/shard_map/sjch,jh->sjc/dot_general | solution.py:34
  275.3 0.0 copy-done.3
  275.3 0.1 fusion.24
  275.4 6.4 %all_to_all.10 = f32[4,4,176]{2,1,0:T(4,128)S(1)} all-to-all(f32[4,4,176]{2,1,0:T(4,128)S(1)} %fusion.24), channel_id=1, replica_groups=mesh['group'=8,'peer'=4] {'peer'}, dimensions={0} | all-to-all | bytes 22528 | tf_op jit(solution)/shard_map/all_to_all | solution.py:38
  281.8 1.8 fusion.10
  283.6 0.6 copy.22
  (3 shorter events, 0.1 us)
Async XLA Ops:
  6.5 4.0 %copy-start = (bf16[384,1024]{1,0:T(8,128)(2,1)S(1)}, bf16[384,1024]{1,0:T(8,128)(2,1)}, u32[]{:S(2)}) copy-start(bf16[384,1024]{1,0:T(8,128)(2,1)} %param.6) | copy-start | bytes 2359300
  6.5 233.5 %all-gather.2.cloned.1.call-start = ((), (), s32[]{:S(2)}) async-start(), calls=%async_computation.2 | async-start | bytes 18874368 | tf_op jit(solution)/shard_map/all_gather | solution.py:29
  15.4 5.3 %copy-start.1 = (bf16[4,256]{1,0:T(4,128)(2,1)S(1)}, bf16[4,256]{1,0:T(4,128)(2,1)}, u32[]{:S(2)}) copy-start(bf16[4,256]{1,0:T(4,128)(2,1)} %param.9) | copy-start | bytes 6148
  15.4 34.7 %copy-start.2 = (bf16[4,256]{1,0:T(4,128)(2,1)S(1)}, bf16[4,256]{1,0:T(4,128)(2,1)}, u32[]{:S(2)}) copy-start(bf16[4,256]{1,0:T(4,128)(2,1)} %param.10) | copy-start | bytes 6148
  15.4 71.2 %all-to-all-start = ((bf16[4,4,176,1024]{3,2,1,0:T(8,128)(2,1)}), bf16[4,4,176,1024]{3,2,1,0:T(8,128)(2,1)}, u32[]{:S(2)}, u32[]{:S(2)}) async-start(bf16[4,4,176,1024]{3,2,1,0:T(8,128)(2,1)} %bitcast.32), calls=%async_computation | async-start | bytes 11534336 | tf_op jit(solution)/shard_map/all_to_all | solution.py:28
  260.6 14.7 %copy-start.3 = (f32[4]{0:T(128)S(1)}, f32[4]{0:T(128)}, u32[]{:S(2)}) copy-start(f32[4]{0:T(128)} %param.11) | copy-start | bytes 52
Sparse Core Ops, SparseCore 0:
  9.5 230.4 all-gather.1
where the time goes:
time: 291 us
  waiting for transfers between devices  163 us (56%)
  blocking collectives  63.1 us (22%)
  matrix products  42 us (14%)
  between operations  13.4 us (5%)
  starting transfers between devices  5.26 us (2%)
  other arithmetic  3.12 us (1%)
    all_gather x1, waiting for transfers between devices, shards(): weight = lax.all_gather(tower_in, 'group', axis=1, tiled=True)  153 us
    all_gather x1, blocking collectives, shards(): hidden_unit_bias = lax.all_gather(tower_bias, 'group', axis=1, tiled=True)  29.4 us
    all_gather x1, blocking collectives, shards(): head_row = lax.all_gather(tower_head, 'group', axis=1, tiled=True)  27.3 us
    dot_general x1, matrix products, shards(): jnp.einsum('sjcd,jhd->sjch', arrived, weight, preferred_element_type=jnp....  20.6 us
    dot_general x1, matrix products, shards(): jnp.einsum('sjch,jh->sjc', hidden, head_row.astype(jnp.float32), precisio...  14.7 us
    all_to_all x1, waiting for transfers between devices, shards(): lax.all_to_all(outgoing, 'peer', split_axis=0, concat_axis=0, tiled=True)  9.23 us
    all_to_all x1, blocking collectives, shards(): lax.all_to_all(logits, 'peer', split_axis=0, concat_axis=0, tiled=True)  6.38 us
  transfers between devices with their start and end apart: 2, of which 2 were waited for; matrix products, arithmetic and copies ran while one was open for 3% of the time, Pallas kernels for 0%

commit v1 on v0

v1 whole, which is shorter than its diff:
```python
import functools

import jax
import jax.numpy as jnp
from jax import lax
from jax.experimental import pallas as pl
from jax.experimental.pallas import tpu as pltpu
from jax.sharding import PartitionSpec as P

MESH = pl.DeviceIdType.MESH
LANES = 128
PIECES = 2
STEP_ROWS = 512
STEP_COLS = 256


def split_of_group(group, peers, weight_bytes, sample_bytes):
    sizes = [f for f in range(1, group + 1) if group % f == 0]

    def cost(f):
        return (f - 1) * weight_bytes + (group // f * peers - 1) * sample_bytes / 2

    return min(sizes, key=cost)


def kernel(
    outer, inner, peers,
    feat_ref, weight_ref, cols_ref, hbias_ref, out_ref,
    x_buf, w_buf, c_buf, part, ret,
    load_sem, x_recv, z_send, y_send, core_send, w_send, w_recv, c_send, c_recv, p_send, p_recv,
):
    rows, depth = feat_ref.shape
    towers, hidden, _ = weight_ref.shape
    piece = rows // PIECES
    ys = peers // 2
    group_at, me = lax.axis_index("group"), lax.axis_index("peer")
    a, i = group_at // inner, group_at % inner
    y, c = me // 2, me % 2
    partner = y * 2 + (1 - c)

    def dev(a_to, i_to, p_to):
        return (a_to * inner + i_to, p_to)

    load_x = pltpu.make_async_copy(
        feat_ref, x_buf.at[a, pl.ds(pl.multiple_of(me * rows, rows), rows)], load_sem.at[0]
    )
    load_w = pltpu.make_async_copy(weight_ref, w_buf.at[i], load_sem.at[1])
    load_c = pltpu.make_async_copy(cols_ref, c_buf.at[i], load_sem.at[2])
    load_x.start()
    load_w.start()
    load_c.start()

    barrier = pltpu.get_barrier_semaphore()
    others = outer * peers - 1

    def greet(k, _):
        at = lax.rem(a * peers + me + k, outer * peers)
        pl.semaphore_signal(
            barrier, inc=1, device_id=dev(at // peers, i, at % peers), device_id_type=MESH
        )
        return 0

    lax.fori_loop(1, others + 1, greet, 0)
    for k in range(1, inner):
        pl.semaphore_signal(
            barrier, inc=1, device_id=dev(a, lax.rem(i + k, inner), me), device_id_type=MESH
        )

    start = jnp.where(a == 0, hbias_ref[...], 0.0)
    for aa in range(outer):
        for pp in range(peers):
            part[aa, pp] = start

    load_x.wait()
    load_w.wait()
    load_c.wait()
    pl.semaphore_wait(barrier, others + inner - 1)

    def x_piece(aa, pp, h):
        return x_buf.at[aa, pl.ds(pl.multiple_of(pp * rows + h * piece, piece), piece)]

    def send_x(aa, pp, h, sem, to):
        ref = x_piece(aa, pp, h)
        return pltpu.make_async_remote_copy(
            src_ref=ref, dst_ref=ref, send_sem=sem, recv_sem=x_recv.at[aa, pp, h],
            device_id=to, device_id_type=MESH,
        )

    def up(aa, h):
        return send_x(aa, me, h, z_send.at[0, aa, h], dev(lax.rem(a + 1, outer), i, me))

    def down(aa, h):
        return send_x(aa, me, h, z_send.at[1, aa, h], dev(lax.rem(a + outer - 1, outer), i, me))

    def across(aa, k, h):
        to = dev(a, i, lax.rem(y + k, ys) * 2 + c)
        return send_x(aa, me, h, y_send.at[aa, k - 1, h], to)

    def sibling(aa, yy, h):
        return send_x(aa, yy * 2 + c, h, core_send.at[aa, yy, h], dev(a, i, partner))

    def arrived(aa, pp, h):
        send_x(aa, pp, h, z_send.at[0, aa, h], dev(a, i, partner)).wait_recv()

    def goes_up(aa):
        return (aa <= a) & (a + 1 < outer)

    def goes_down(aa):
        return (aa >= a) & (a > 0)

    def send_w(k, t):
        return pltpu.make_async_remote_copy(
            src_ref=w_buf.at[i, t], dst_ref=w_buf.at[i, t],
            send_sem=w_send.at[k - 1, t], recv_sem=w_recv.at[i, t],
            device_id=dev(a, lax.rem(i + k, inner), me), device_id_type=MESH,
        )

    def send_c(k):
        return pltpu.make_async_remote_copy(
            src_ref=c_buf.at[i], dst_ref=c_buf.at[i],
            send_sem=c_send.at[k - 1], recv_sem=c_recv.at[i],
            device_id=dev(a, lax.rem(i + k, inner), me), device_id_type=MESH,
        )

    def nth(j):
        low = jnp.minimum(a, outer - 1 - a)
        near = jnp.where(j % 2 == 1, a - (j + 1) // 2, a + j // 2)
        far = jnp.where(a < outer - 1 - a, j, outer - 1 - j)
        return jnp.where(j <= 2 * low, near, far)

    def spread(aa, first):
        for h in range(PIECES):
            if not first:
                arrived(aa, me, h)
            pl.when(goes_up(aa))(lambda h=h: up(aa, h).start())
            pl.when(goes_down(aa))(lambda h=h: down(aa, h).start())
            for k in range(1, ys):
                across(aa, k, h).start()
            sibling(aa, y, h).start()

    def pass_on(aa):
        for k in range(1, ys):
            yy = lax.rem(y + k, ys)
            for h in range(PIECES):
                arrived(aa, yy * 2 + c, h)
                sibling(aa, yy, h).start()

    def settle(aa, yy):
        for h in range(PIECES):
            arrived(aa, yy * 2 + (1 - c), h)

    n_steps, per_step, _ = hbias_ref.shape
    span = 2 * rows
    cols = STEP_COLS if span % STEP_COLS == 0 else span

    def compute(aa, yy, ii):
        def body(s, _):
            t0 = s * per_step
            w = w_buf[ii, pl.ds(t0, per_step)].reshape(per_step * hidden, depth)
            bias = c_buf[ii, 0, pl.ds(t0, per_step)].reshape(per_step * hidden, LANES)
            head = c_buf[ii, 1, pl.ds(t0, per_step)].reshape(per_step * hidden, LANES)
            bias = bias.astype(jnp.float32)
            head = head.astype(jnp.float32)
            for n in range(span // cols):
                at = pl.ds(pl.multiple_of(yy * span + n * cols, LANES), cols)
                pre = lax.dot_general(
                    w, x_buf[aa, at], (((1,), (1,)), ((), ())),
                    preferred_element_type=jnp.float32,
                )
                for l in range(cols // LANES):
                    tile = n * cols + l * LANES
                    v = jnp.maximum(pre[:, l * LANES : (l + 1) * LANES] + bias, 0.0) * head
                    for t in range(per_step):
                        total = jnp.sum(v[t * hidden : (t + 1) * hidden], axis=0, keepdims=True)
                        lane = pl.ds(tile % rows, LANES)
                        part[aa, yy * 2 + tile // rows, s, pl.ds(t, 1), lane] += total
            return 0

        lax.fori_loop(0, n_steps, body, 0)

    def send_part(aa, pp):
        return pltpu.make_async_remote_copy(
            src_ref=part.at[aa, pp], dst_ref=ret.at[a, me],
            send_sem=p_send.at[aa, pp], recv_sem=p_recv.at[a, me],
            device_id=dev(aa, i, pp), device_id_type=MESH,
        )

    def give_back(aa, yy):
        for cc in range(2):
            pp = yy * 2 + cc
            mine = (aa == a) & (pp == me)
            pl.when(jnp.logical_not(mine))(lambda pp=pp: send_part(aa, pp).start())

    spread(a, True)
    for k in range(1, inner):
        send_c(k).start()
        for t in range(towers):
            send_w(k, t).start()

    settle(a, y)
    compute(a, y, i)

    def round_(j, _):
        aa, before = nth(j), nth(j - 1)
        spread(aa, False)
        pass_on(before)
        for k in range(1, ys):
            yy = lax.rem(y + k, ys)
            settle(before, yy)
            compute(before, yy, i)
        settle(aa, y)
        compute(aa, y, i)
        return 0

    lax.fori_loop(1, outer, round_, 0)

    def w_arrived(k):
        ii = lax.rem(i + k, inner)
        pltpu.make_async_remote_copy(
            src_ref=c_buf.at[ii], dst_ref=c_buf.at[ii], send_sem=c_send.at[0],
            recv_sem=c_recv.at[ii], device_id=dev(a, ii, me), device_id_type=MESH,
        ).wait_recv()
        for t in range(towers):
            pltpu.make_async_remote_copy(
                src_ref=w_buf.at[ii, t], dst_ref=w_buf.at[ii, t], send_sem=w_send.at[0, t],
                recv_sem=w_recv.at[ii, t], device_id=dev(a, ii, me), device_id_type=MESH,
            ).wait_recv()

    for k in range(1, inner):
        w_arrived(k)

    def rest(aa, yy):
        def one(k, _):
            compute(aa, yy, lax.rem(i + k, inner))
            return 0

        lax.fori_loop(1, inner, one, 0)
        give_back(aa, yy)

    def early(q, _):
        j, k = q // ys, q % ys
        rest(nth(j), lax.rem(y + k, ys))
        return 0

    last = nth(outer - 1)
    lax.fori_loop(0, (outer - 1) * ys, early, 0)
    rest(last, y)
    pass_on(last)
    for k in range(1, ys):
        yy = lax.rem(y + k, ys)
        settle(last, yy)
        compute(last, yy, i)
        rest(last, yy)

    def landed(aa, pp):
        pltpu.make_async_remote_copy(
            src_ref=part.at[aa, pp], dst_ref=ret.at[aa, pp], send_sem=p_send.at[aa, pp],
            recv_sem=p_recv.at[aa, pp], device_id=dev(a, i, partner), device_id_type=MESH,
        ).wait_recv()

    ret[a, me] = part[a, me]
    for aa in range(outer):
        for pp in range(peers):
            mine = (a == aa) & (me == pp)
            pl.when(jnp.logical_not(mine))(lambda aa=aa, pp=pp: landed(aa, pp))
    for pp in range(peers):
        total = ret[0, pp]
        for aa in range(1, outer):
            total += ret[aa, pp]
        out_ref[pp] = total

    for aa in range(outer):
        for h in range(PIECES):
            pl.when(goes_up(aa))(lambda aa=aa, h=h: up(aa, h).wait_send())
            pl.when(goes_down(aa))(lambda aa=aa, h=h: down(aa, h).wait_send())
            for k in range(1, ys):
                across(aa, k, h).wait_send()
            for yy in range(ys):
                sibling(aa, yy, h).wait_send()
        for pp in range(peers):
            mine = (a == aa) & (me == pp)
            pl.when(jnp.logical_not(mine))(lambda aa=aa, pp=pp: send_part(aa, pp).wait_send())
    for k in range(1, inner):
        send_c(k).wait_send()
        for t in range(towers):
            send_w(k, t).wait_send()


def shards(features, task_mask, tower_in, tower_bias, tower_head, head_bias):
    peers, group = lax.axis_size("peer"), lax.axis_size("group")
    rows, depth = features.shape
    towers, hidden, _ = tower_in.shape
    inner = split_of_group(group, peers, tower_in.size, features.size)
    outer = group // inner
    ys = peers // 2
    columns = jnp.stack([tower_bias, tower_head])[..., None]
    columns = jnp.broadcast_to(columns, (2, towers, hidden, LANES))
    per_step = max(n for n in range(1, towers + 1) if towers % n == 0 and n * hidden <= STEP_ROWS)
    steps = (towers // per_step, per_step)
    start = jnp.broadcast_to(head_bias.reshape(steps)[..., None], (*steps, rows))
    dma = pltpu.SemaphoreType.DMA
    logits = pl.pallas_call(
        functools.partial(kernel, outer, inner, peers),
        out_shape=jax.ShapeDtypeStruct((peers, *steps, rows), jnp.float32),
        in_specs=[pl.BlockSpec(memory_space=pl.ANY)] * 3
        + [pl.BlockSpec(memory_space=pltpu.VMEM)],
        out_specs=pl.BlockSpec(memory_space=pltpu.VMEM),
        scratch_shapes=[
            pltpu.VMEM((outer, peers * rows, depth), features.dtype),
            pltpu.VMEM((inner, towers, hidden, depth), tower_in.dtype),
            pltpu.VMEM((inner, 2, towers, hidden, LANES), tower_bias.dtype),
            pltpu.VMEM((outer, peers, *steps, rows), jnp.float32),
            pltpu.VMEM((outer, peers, *steps, rows), jnp.float32),
            dma((3,)),
            dma((outer, peers, PIECES)),
            dma((2, outer, PIECES)),
            dma((outer, max(1, ys - 1), PIECES)),
            dma((outer, ys, PIECES)),
            dma((max(1, inner - 1), towers)),
            dma((inner, towers)),
            dma((max(1, inner - 1),)),
            dma((inner,)),
            dma((outer, peers)),
            dma((outer, peers)),
        ],
        compiler_params=pltpu.CompilerParams(
            collective_id=0, has_side_effects=True, vmem_limit_bytes=60 * 1024 * 1024
        ),
    )(features, tower_in, columns, start)
    tasks = jnp.arange(peers * towers, dtype=jnp.int32)
    bits = (task_mask[:, None] >> tasks[None, :]) & 1
    return jnp.where(bits == 1, logits.reshape(peers * towers, rows).T, 0.0)


def solution(mesh):
    placed = (
        P(("group", "peer"), None),
        P(("group", "peer")),
        P("peer", "group", None),
        P("peer", "group"),
        P("peer", "group"),
        P("peer"),
    )
    return jax.shard_map(
        shards, mesh=mesh, in_specs=placed, out_specs=P(("group", "peer"), None), check_vma=False
    )
```

time: 291 us -> 103 us (0.35)
  waiting for transfers between devices: 163 us -> 0 us
  Pallas kernels: 0 us -> 98.5 us
  blocking collectives: 63.1 us -> 0 us
  matrix products: 42 us -> 0 us
  between operations: 13.4 us -> 0.02 us
  starting transfers between devices: 5.26 us -> 0 us
    all_gather x1 -> x0, waiting for transfers between devices: 153 us -> none  [shards(): weight = lax.all_gather(tower_in, 'group', axis=1, tiled=True)]
    pallas_call x0 -> x1, Pallas kernels: none -> 98.5 us  [shards(): pl.pallas_call(functools.partial(kernel, outer, inner, peers), out_shape=...]
    all_gather x2 -> x0, blocking collectives: 56.7 us -> none  [the longest x1 29.4 us: shards(): hidden_unit_bias = lax.all_gather(tower_bias, 'group', axis=1, tiled=True)]
    dot_general x4 -> x0, matrix products: 42 us -> none  [the longest x1 20.6 us: shards(): jnp.einsum('sjcd,jhd->sjch', arrived, weight, preferred_element_type=jnp....]
    all_to_all x1 -> x0, waiting for transfers between devices: 9.23 us -> none  [shards(): lax.all_to_all(outgoing, 'peer', split_axis=0, concat_axis=0, tiled=True)]
    all_to_all x1 -> x0, blocking collectives: 6.38 us -> none  [shards(): lax.all_to_all(logits, 'peer', split_axis=0, concat_axis=0, tiled=True)]
    all_to_all x1 -> x0, starting transfers between devices: 5.26 us -> none  [shards(): lax.all_to_all(outgoing, 'peer', split_axis=0, concat_axis=0, tiled=True)]
  transfers between devices with their start and end apart: 2 -> 0, of which waited for: 2 -> 0; matrix products, arithmetic and copies ran while one was open for 3% -> 0% of each run, Pallas kernels for 0% -> 0%
where the time goes in v1:
time: 103 us
  Pallas kernels  98.5 us (96%)
  local copies, waits for them, and re-layouts  3.29 us (3%)
  other arithmetic  1.32 us (1%)
    pallas_call x1, Pallas kernels, shards(): pl.pallas_call(functools.partial(kernel, outer, inner, peers), out_shape=...  98.5 us

profile of v1, /device:TPU:0, one launch (start us, length us, event | category | flops | bytes accessed | tf_op | source)
XLA Modules:
  0.0 103.2 jit_solution(6187657198243536076)
XLA Ops:
  0.0 0.0 copy-start
  0.0 0.7 broadcast_in_dim.20
  0.8 0.7 pad_maximum_fusion
  1.5 0.7 broadcast_in_dim.21.hbias_ref
  2.1 1.1 %broadcast_in_dim.9.cols_ref = bf16[2,4,256,128]{3,2,1,0:T(8,128)(2,1)} broadcast(bf16[2,4,256]{2,1,0:T(4,128)(2,1)S(1)} %pad_maximum_fusion), dimensions={0,1,2} | broadcast | bytes 528384 | tf_op jit(solution)/shard_map/broadcast_in_dim | solution.py:297
  3.2 98.5 %shard_map.64 = f32[4,2,2,384]{3,2,1,0:T(2,128)} custom-call(bf16[384,1024]{1,0:T(8,128)(2,1)} %feat_ref.1, bf16[4,256,1024]{2,1,0:T(8,128)(2,1)} %weight_ref.1, bf16[2,4,256,128]{3,2,1,0:T(8,128)(2,1)} %broadcast_in_dim.9.cols_ref, f32[2,2,384]{2,1,0:T(2,128)} %broadcast_in_dim.21.hbias_ref), custom_call_target="tpu_custom_call" | custom-call | tf_op jit(solution)/shard_map/pallas_call | solution.py:302
  101.8 0.8 reshape.6
  102.5 0.0 copy-done
  102.6 0.6 bitcast_select_fusion
Async XLA Ops:
  0.0 102.5 %copy-start = (s32[384]{0:T(512)S(1)}, s32[384]{0:T(512)}, u32[]{:S(2)}) copy-start(s32[384]{0:T(512)} %param.7) | copy-start | bytes 4612

commit v2 on v1

v2 whole, which is shorter than its diff:
```python
import functools

import jax
import jax.numpy as jnp
from jax import lax
from jax.experimental import pallas as pl
from jax.experimental.pallas import tpu as pltpu
from jax.sharding import PartitionSpec as P

MESH = pl.DeviceIdType.MESH
LANES = 128
PIECE_ROWS = 64
FIRST = 0
STEP_COLS = 256


def split_of_group(group, peers, weight_bytes, sample_bytes):
    sizes = [f for f in range(1, group + 1) if group % f == 0]

    def cost(f):
        return (f - 1) * weight_bytes + (group // f * peers - 1) * sample_bytes / 2

    return min(sizes, key=cost)


def kernel(
    outer, inner, peers,
    feat_ref, weight_ref, bias_ref, head_ref, hbias_ref, out_ref,
    x_buf, w_buf, b_buf, c_buf, part, ret,
    load_sem, x_recv, z_send, f_send, y_send, core_send, w_send, w_recv, b_send, b_recv,
    p_send, p_recv,
):
    rows, depth = feat_ref.shape
    towers, hidden, _ = weight_ref.shape
    piece = PIECE_ROWS
    pieces = rows // piece
    ys = peers // 2
    group_at, me = lax.axis_index("group"), lax.axis_index("peer")
    a, i = group_at // inner, group_at % inner
    y, c = me // 2, me % 2
    partner = y * 2 + (1 - c)

    def dev(a_to, i_to, p_to):
        return (a_to * inner + i_to, p_to)

    load_x = pltpu.make_async_copy(
        feat_ref, x_buf.at[a, pl.ds(pl.multiple_of(me * rows, rows), rows)], load_sem.at[0]
    )
    load_w = pltpu.make_async_copy(weight_ref, w_buf.at[i], load_sem.at[1])
    load_b = pltpu.make_async_copy(bias_ref, b_buf.at[i, 0], load_sem.at[2])
    load_h = pltpu.make_async_copy(head_ref, b_buf.at[i, 1], load_sem.at[3])
    load_x.start()
    load_w.start()
    load_b.start()
    load_h.start()

    barrier = pltpu.get_barrier_semaphore()
    others = outer * peers - 1

    def greet(k, _):
        at = lax.rem(a * peers + me + k, outer * peers)
        pl.semaphore_signal(
            barrier, inc=1, device_id=dev(at // peers, i, at % peers), device_id_type=MESH
        )
        return 0

    lax.fori_loop(1, others + 1, greet, 0)
    for k in range(1, inner):
        pl.semaphore_signal(
            barrier, inc=1, device_id=dev(a, lax.rem(i + k, inner), me), device_id_type=MESH
        )

    for t in range(towers):
        start = jnp.where(a == 0, hbias_ref[t], 0.0)
        for aa in range(outer):
            for pp in range(peers):
                part[aa, pp, pl.ds(t, 1)] = jnp.full((1, rows), start, jnp.float32)

    load_x.wait()
    load_w.wait()
    load_b.wait()
    load_h.wait()
    pl.semaphore_wait(barrier, others + inner - 1)

    def x_piece(aa, pp, h):
        return x_buf.at[aa, pl.ds(pl.multiple_of(pp * rows + h * piece, piece), piece)]

    def send_x(aa, pp, h, sem, to):
        ref = x_piece(aa, pp, h)
        return pltpu.make_async_remote_copy(
            src_ref=ref, dst_ref=ref, send_sem=sem, recv_sem=x_recv.at[aa, pp, h],
            device_id=to, device_id_type=MESH,
        )

    def up(aa, h):
        return send_x(aa, me, h, z_send.at[0, aa, h], dev(lax.rem(a + 1, outer), i, me))

    def down(aa, h):
        return send_x(aa, me, h, z_send.at[1, aa, h], dev(lax.rem(a + outer - 1, outer), i, me))

    def across(aa, k, h):
        to = dev(a, i, lax.rem(y + k, ys) * 2 + c)
        return send_x(aa, me, h, y_send.at[aa, k - 1, h], to)

    def sibling(aa, yy, h):
        return send_x(aa, yy * 2 + c, h, core_send.at[aa, yy, h], dev(a, i, partner))

    def arrived(aa, pp, h):
        send_x(aa, pp, h, z_send.at[0, aa, h], dev(a, i, partner)).wait_recv()

    def goes_up(aa):
        return (aa <= a) & (a + 1 < outer)

    def goes_down(aa):
        return (aa >= a) & (a > 0)

    def send_w(k, t):
        return pltpu.make_async_remote_copy(
            src_ref=w_buf.at[i, t], dst_ref=w_buf.at[i, t],
            send_sem=w_send.at[k - 1, t], recv_sem=w_recv.at[i, t],
            device_id=dev(a, lax.rem(i + k, inner), me), device_id_type=MESH,
        )

    def send_b(k):
        return pltpu.make_async_remote_copy(
            src_ref=b_buf.at[i], dst_ref=b_buf.at[i],
            send_sem=b_send.at[k - 1], recv_sem=b_recv.at[i],
            device_id=dev(a, lax.rem(i + k, inner), me), device_id_type=MESH,
        )

    def columns(ii):
        diagonal = lax.broadcasted_iota(jnp.int32, (hidden, hidden), 0) == (
            lax.broadcasted_iota(jnp.int32, (hidden, hidden), 1)
        )
        for w in range(2):
            both = b_buf[ii, w].astype(jnp.float32)
            for t in range(towers):
                picked = jnp.where(diagonal, both[t : t + 1], 0.0)
                column = jnp.sum(picked, axis=1, keepdims=True)
                c_buf[ii, w, t] = jnp.broadcast_to(column, (hidden, LANES))

    def nth(j):
        low = jnp.minimum(a, outer - 1 - a)
        near = jnp.where(j % 2 == 1, a - (j + 1) // 2, a + j // 2)
        far = jnp.where(a < outer - 1 - a, j, outer - 1 - j)
        return jnp.where(j <= 2 * low, near, far)

    def cross_first(aa, k, d):
        pp = lax.rem(y + k, ys) * 2 + c
        to = dev(lax.rem(a + outer + 1 - 2 * d, outer), i, me)
        return send_x(aa, pp, FIRST, f_send.at[d, aa, k - 1], to)

    def spread(aa, h, own):
        if not own:
            arrived(aa, me, h)
        pl.when(goes_up(aa))(lambda: up(aa, h).start())
        pl.when(goes_down(aa))(lambda: down(aa, h).start())
        if own or h != FIRST:
            for k in range(1, ys):
                across(aa, k, h).start()
        sibling(aa, y, h).start()

    def pass_on(aa, h):
        for k in range(1, ys):
            yy = lax.rem(y + k, ys)
            arrived(aa, yy * 2 + c, h)
            if h == FIRST:
                pl.when(goes_up(aa))(lambda k=k: cross_first(aa, k, 0).start())
                pl.when(goes_down(aa))(lambda k=k: cross_first(aa, k, 1).start())
            sibling(aa, yy, h).start()

    def settle(aa, yy):
        for h in range(pieces):
            arrived(aa, yy * 2 + (1 - c), h)

    span = 2 * rows
    cols = STEP_COLS if span % STEP_COLS == 0 else span

    def compute(aa, yy, ii, t0, t1):
        count = (t1 - t0) * hidden
        w = w_buf[ii, t0:t1].reshape(count, depth)
        bias = c_buf[ii, 0, t0:t1].reshape(count, LANES)
        head = c_buf[ii, 1, t0:t1].reshape(count, LANES)
        for n in range(span // cols):
            at = pl.ds(pl.multiple_of(yy * span + n * cols, LANES), cols)
            pre = lax.dot_general(
                w, x_buf[aa, at], (((1,), (1,)), ((), ())),
                preferred_element_type=jnp.float32,
            )
            for l in range(cols // LANES):
                tile = n * cols + l * LANES
                lane = pl.ds(tile % rows, LANES)
                v = jnp.maximum(pre[:, l * LANES : (l + 1) * LANES] + bias, 0.0) * head
                for t in range(t1 - t0):
                    total = jnp.sum(v[t * hidden : (t + 1) * hidden], axis=0, keepdims=True)
                    part[aa, yy * 2 + tile // rows, pl.ds(t0 + t, 1), lane] += total

    def send_part(aa, pp):
        return pltpu.make_async_remote_copy(
            src_ref=part.at[aa, pp], dst_ref=ret.at[a, me],
            send_sem=p_send.at[aa, pp], recv_sem=p_recv.at[a, me],
            device_id=dev(aa, i, pp), device_id_type=MESH,
        )

    def give_back(aa, yy):
        for cc in range(2):
            pp = yy * 2 + cc
            mine = (aa == a) & (pp == me)
            pl.when(jnp.logical_not(mine))(lambda pp=pp: send_part(aa, pp).start())

    def pair(u):
        return nth(u // ys), lax.rem(y + u % ys, ys)

    far = max(inner - 1, 1)
    half = towers // 2

    def own_jobs(u1):
        for u in range(done[0], u1):
            settle(*pair(u))

        def job(u, _):
            compute(*pair(u), i, 0, towers)
            return 0

        if u1 > done[0]:
            lax.fori_loop(done[0], u1, job, 0)
        done[0] = max(done[0], u1)

    def far_jobs(v0, v1, t0, t1):
        def job(q, _):
            compute(*pair(q // far), lax.rem(i + 1 + q % far, inner), t0, t1)
            return 0

        if v1 > v0 and inner > 1:
            lax.fori_loop(v0 * far, v1 * far, job, 0)
        if t1 == towers:
            for v in range(v0, v1):
                give_back(*pair(v))

    def low_jobs(v1):
        v1 = min(v1, done[0])
        far_jobs(done[1], v1, 0, half)
        done[1] = max(done[1], v1)

    def high_jobs(v1):
        v1 = min(v1, done[1])
        far_jobs(done[2], v1, half, towers)
        done[2] = max(done[2], v1)

    for h in range(pieces):
        spread(a, h, True)
    for k in range(1, inner):
        send_b(k).start()
        for t in range(towers):
            send_w(k, t).start()
    columns(i)

    def weights_arrived(part_of):
        if part_of in got:
            return
        got.add(part_of)
        for k in range(1, inner):
            ii = lax.rem(i + k, inner)
            if part_of == 0:
                pltpu.make_async_remote_copy(
                    src_ref=b_buf.at[ii], dst_ref=b_buf.at[ii], send_sem=b_send.at[0],
                    recv_sem=b_recv.at[ii], device_id=dev(a, ii, me), device_id_type=MESH,
                ).wait_recv()
                columns(ii)
            for t in range(half) if part_of == 0 else range(half, towers):
                pltpu.make_async_remote_copy(
                    src_ref=w_buf.at[ii, t], dst_ref=w_buf.at[ii, t], send_sem=w_send.at[0, t],
                    recv_sem=w_recv.at[ii, t], device_id=dev(a, ii, me), device_id_type=MESH,
                ).wait_recv()

    pairs = outer * ys
    done, got = [0, 0, 0], set()
    own_jobs(1)
    for j in range(1, outer):
        aa, before = nth(j), nth(j - 1)
        passed = 0
        window = pieces if j == 1 else max(1, pieces - 2)
        for h in range(pieces):
            spread(aa, h, False)
            upto = min(pieces, -(-pieces * (h + 1) // window))
            for g in range(passed, upto):
                pass_on(before, g)
            passed = upto
            if upto == pieces:
                own_jobs(j * ys)
            late = h >= window - 1
            if (j == outer - 2 and late) or j == outer - 1:
                weights_arrived(0)
                low_jobs(done[1] + 1)
            if j == outer - 1 and late:
                weights_arrived(1)
                high_jobs(done[2] + 2)
        if j < outer - 1:
            own_jobs(j * ys + 1)
    weights_arrived(0)
    weights_arrived(1)
    last = nth(outer - 1)
    for h in range(pieces - 2):
        pass_on(last, h)
    own_jobs((outer - 1) * ys + 1)
    for h in range(max(0, pieces - 2), pieces):
        pass_on(last, h)
    low_jobs(done[0])
    high_jobs(done[1])
    for u in range(done[0], pairs):
        own_jobs(u + 1)
        far_jobs(u, u + 1, 0, towers)

    def landed(aa, pp):
        pltpu.make_async_remote_copy(
            src_ref=part.at[aa, pp], dst_ref=ret.at[aa, pp], send_sem=p_send.at[aa, pp],
            recv_sem=p_recv.at[aa, pp], device_id=dev(a, i, partner), device_id_type=MESH,
        ).wait_recv()

    ret[a, me] = part[a, me]
    for aa in range(outer):
        for pp in range(peers):
            mine = (a == aa) & (me == pp)
            pl.when(jnp.logical_not(mine))(lambda aa=aa, pp=pp: landed(aa, pp))
    for pp in range(peers):
        total = ret[0, pp]
        for aa in range(1, outer):
            total += ret[aa, pp]
        out_ref[pp] = total

    for aa in range(outer):
        for h in range(pieces):
            pl.when(goes_up(aa))(lambda aa=aa, h=h: up(aa, h).wait_send())
            pl.when(goes_down(aa))(lambda aa=aa, h=h: down(aa, h).wait_send())
            for k in range(1, ys):
                sent = (a == aa) | (h != FIRST)
                pl.when(sent)(lambda aa=aa, k=k, h=h: across(aa, k, h).wait_send())
            for yy in range(ys):
                sibling(aa, yy, h).wait_send()
        for k in range(1, ys):
            pl.when(goes_up(aa))(lambda aa=aa, k=k: cross_first(aa, k, 0).wait_send())
            pl.when(goes_down(aa))(lambda aa=aa, k=k: cross_first(aa, k, 1).wait_send())
        for pp in range(peers):
            mine = (a == aa) & (me == pp)
            pl.when(jnp.logical_not(mine))(lambda aa=aa, pp=pp: send_part(aa, pp).wait_send())
    for k in range(1, inner):
        send_b(k).wait_send()
        for t in range(towers):
            send_w(k, t).wait_send()


def shards(features, task_mask, tower_in, tower_bias, tower_head, head_bias):
    peers, group = lax.axis_size("peer"), lax.axis_size("group")
    rows, depth = features.shape
    towers, hidden, _ = tower_in.shape
    inner = split_of_group(group, peers, tower_in.size, features.size)
    outer = group // inner
    ys = peers // 2
    pieces = rows // PIECE_ROWS
    dma = pltpu.SemaphoreType.DMA
    logits = pl.pallas_call(
        functools.partial(kernel, outer, inner, peers),
        out_shape=jax.ShapeDtypeStruct((peers, towers, rows), jnp.float32),
        in_specs=[pl.BlockSpec(memory_space=pl.ANY)] * 4
        + [pl.BlockSpec(memory_space=pltpu.SMEM)],
        out_specs=pl.BlockSpec(memory_space=pltpu.VMEM),
        scratch_shapes=[
            pltpu.VMEM((outer, peers * rows, depth), features.dtype),
            pltpu.VMEM((inner, towers, hidden, depth), tower_in.dtype),
            pltpu.VMEM((inner, 2, towers, hidden), tower_bias.dtype),
            pltpu.VMEM((inner, 2, towers, hidden, LANES), jnp.float32),
            pltpu.VMEM((outer, peers, towers, rows), jnp.float32),
            pltpu.VMEM((outer, peers, towers, rows), jnp.float32),
            dma((4,)),
            dma((outer, peers, pieces)),
            dma((2, outer, pieces)),
            dma((2, outer, max(1, ys - 1))),
            dma((outer, max(1, ys - 1), pieces)),
            dma((outer, ys, pieces)),
            dma((max(1, inner - 1), towers)),
            dma((inner, towers)),
            dma((max(1, inner - 1),)),
            dma((inner,)),
            dma((outer, peers)),
            dma((outer, peers)),
        ],
        compiler_params=pltpu.CompilerParams(
            collective_id=0, has_side_effects=True, vmem_limit_bytes=60 * 1024 * 1024
        ),
    )(features, tower_in, tower_bias, tower_head, head_bias)
    tasks = jnp.arange(peers * towers, dtype=jnp.int32)
    bits = (task_mask[:, None] >> tasks[None, :]) & 1
    return jnp.where(bits == 1, logits.reshape(peers * towers, rows).T, 0.0)


def solution(mesh):
    placed = (
        P(("group", "peer"), None),
        P(("group", "peer")),
        P("peer", "group", None),
        P("peer", "group"),
        P("peer", "group"),
        P("peer"),
    )
    return jax.shard_map(
        shards, mesh=mesh, in_specs=placed, out_specs=P(("group", "peer"), None), check_vma=False
    )
```

time: 103 us -> 93.3 us (0.906)
  Pallas kernels: 98.5 us -> 91.7 us
  local copies, waits for them, and re-layouts: 3.29 us -> 0.75 us
    pallas_call x1, Pallas kernels: 98.5 us -> 91.7 us  [shards(): pl.pallas_call(functools.partial(kernel, outer, inner, peers), out_shape=...]
    broadcast_in_dim x3 -> x0, local copies, waits for them, and re-layouts: 2.53 us -> none  [the longest x2 1.41 us: shards(): jnp.broadcast_to(head_bias.reshape(steps)[..., None], (*steps, rows))]
where the time goes in v2:
time: 93.3 us; the launch traced here: 93 us
  Pallas kernels  91.7 us (98%)
    pallas_call x1, Pallas kernels, shards(): pl.pallas_call(functools.partial(kernel, outer, inner, peers), out_shape=...  91.7 us

profile of v2, /device:TPU:0, one launch (start us, length us, event | category | flops | bytes accessed | tf_op | source)
XLA Modules:
  0.0 93.0 jit_solution(11223122420960892658)
XLA Ops:
  0.0 0.0 copy-start
  0.0 91.7 %shard_map.64 = f32[4,4,384]{2,1,0:T(4,128)} custom-call(bf16[384,1024]{1,0:T(8,128)(2,1)} %feat_ref.1, bf16[4,256,1024]{2,1,0:T(8,128)(2,1)} %weight_ref.1, bf16[4,256]{1,0:T(4,128)(2,1)} %bias_ref.1, bf16[4,256]{1,0:T(4,128)(2,1)} %head_ref.1, f32[4]{0:T(128)} %hbias_ref.1), custom_call_target="tpu_custom_call" | custom-call | tf_op jit(solution)/shard_map/pallas_call | solution.py:361
  91.7 0.8 reshape.4
  92.4 0.0 copy-done
  92.4 0.6 bitcast_select_fusion
Async XLA Ops:
  0.0 92.4 %copy-start = (s32[384]{0:T(512)S(1)}, s32[384]{0:T(512)}, u32[]{:S(2)}) copy-start(s32[384]{0:T(512)} %param.7) | copy-start | bytes 4612
